TPU v7x, 32 devices: a whole 2x2x4 slice. The times are simulated.
32 devices in a mesh: grp: 4 (over y, x), bal: 8 (over z, core).
Axes of the slice: x: 2, y: 2, z: 4, core: 2. Of those that a mesh axis runs over, the one named last changes fastest.
Arguments:
- tracers: float32 [2, 64, 16, 2048], P(None, None, 'grp', 'bal'), may hold values from -6 to 6
- winds: bfloat16 [2, 64, 16, 2048], P(None, None, 'grp', 'bal'), may hold values from -16 to 16
- node_mass: float32 [16, 2048], P('grp', 'bal'), may hold values from 0.07 to 5.6
- column_cost: int32 [8, 1024], P('grp', 'bal'), may hold values from 1 to 3, as said below
- weight_in: bfloat16 [256, 1024], replicated, may hold values from -0.375 to 0.375
- weight_out: bfloat16 [1024, 256], replicated, may hold values from -0.1875 to 0.1875
Outputs:
- tracers_next: float32 [2, 64, 16, 2048], P(None, None, 'grp', 'bal')
- columns_out: bfloat16 [4, 64, 8, 1024], P(None, None, 'grp', 'bal')
Inputs may be any that keep to these rules, and one draw needn't show every extreme that they name: `column_cost`: among the columns of one index of grp (rows 2 * g to 2 * g + 1 of all columns), exactly a quarter have cost 3 and exactly a quarter cost 2.
All inputs are finite; a program needn't handle non-finite values.
Results may differ from a plain program's by a relative error of at most 0.008.
Values may be sent and summed in bfloat16 or wider, within the bound.
A program may use at most 64 MiB of HBM per device.

v0:
```python
import functools

import jax
import jax.numpy as jnp
import numpy as np
from jax import lax
from jax.experimental import pallas as pl
from jax.experimental.pallas import tpu as pltpu
from jax.sharding import PartitionSpec as P

MESH = pl.DeviceIdType.MESH
time_step = 0.02
remap_ints = ((9.0, 8.0, 3.0, 0.0), (0.0, 3.0, 8.0, 9.0))
gll_points = (-1.0, -0.4472135954999579, 0.4472135954999579, 1.0)

DIRS = ((1, 0), (-1, 0), (0, 1), (0, -1), (1, 1), (1, -1), (-1, 1), (-1, -1))
FROM_UP, FROM_DOWN, FROM_LEFT, FROM_RIGHT = 0, 1, 2, 3
FROM_UL, FROM_UR, FROM_DL, FROM_DR = 4, 5, 6, 7


def gll_matrix():
    points = gll_points
    matrix = np.zeros((4, 4))
    for i in range(4):
        for j in range(4):
            if i == j:
                matrix[i, i] = 2.0 * sum(
                    1.0 / (points[i] - points[k]) for k in range(4) if k != i
                )
            else:
                num = den = 1.0
                for k in range(4):
                    if k != i:
                        num *= points[i] - points[k]
                    if k != j:
                        den *= points[j] - points[k]
                matrix[i, j] = 2.0 * num / (den * (points[i] - points[j]))
    return matrix


def constants(across):
    elements = across // 4
    eye = np.eye(elements)
    along = np.kron(eye, gll_matrix().T).astype(np.float32)
    high = along.astype(jnp.bfloat16)
    low = (along - high.astype(np.float32)).astype(jnp.bfloat16)
    remap = np.kron(eye, np.array(remap_ints).T).astype(jnp.bfloat16)
    pick = np.zeros((4, 8, across), np.float32)
    for a in range(4):
        pick[a, a, 0] = 1.0
        pick[a, 4 + a, across - 1] = 1.0
    place = np.zeros((4, 48, across), np.float32)
    for a in range(4):
        place[a, 8 * 0 + 4 + a, 0] = 1.0
        place[a, 8 * 1 + a, across - 1] = 1.0
    place[0, 8 * 2 + 7, 0] = 1.0
    place[0, 8 * 3 + 3, across - 1] = 1.0
    place[3, 8 * 4 + 4, 0] = 1.0
    place[3, 8 * 5 + 0, across - 1] = 1.0
    return high, low, remap, pick.astype(jnp.bfloat16), place.astype(jnp.bfloat16)


def dot(a, b):
    return jnp.dot(a, b, preferred_element_type=jnp.float32)


def split(value):
    high = value.astype(jnp.bfloat16)
    return high, (value - high.astype(jnp.float32)).astype(jnp.bfloat16)


def kernel(
    sizes,
    tracers_hbm, winds_hbm, mass_hbm,
    dhigh_hbm, dlow_hbm, remap_hbm, pick_hbm, place_hbm,
    next_hbm, start_ref,
    tracers_ref, winds_ref, mass_ref,
    dhigh_ref, dlow_ref, remap_ref, pick_ref, place_ref,
    weighted, next_ref, rows_out, rows_in, ends_out, ends_in,
    mass_in, local_sem, store_sem, send_sem, recv_sem,
):
    n_grp, n_bal = sizes
    levels, across = winds_ref.shape[1], winds_ref.shape[3]
    grp, bal = lax.axis_index("grp"), lax.axis_index("bal")

    def peer(i):
        dg, db = DIRS[i]
        return (lax.rem(grp + dg + n_grp, n_grp), lax.rem(bal + db + n_bal, n_bal))

    barrier = pltpu.get_barrier_semaphore()
    for i in range(8):
        pl.semaphore_signal(barrier, inc=1, device_id=peer(i), device_id_type=MESH)

    def load(src, dst, slot):
        copy = pltpu.make_async_copy(src, dst, local_sem.at[slot])
        copy.start()
        return copy

    load_rows = [load(tracers_hbm.at[:, :, a, :], tracers_ref.at[a], a) for a in range(4)]
    load_high = load(dhigh_hbm, dhigh_ref, 4)
    load_low = load(dlow_hbm, dlow_ref, 5)
    load_winds = load(winds_hbm, winds_ref, 6)
    load_mass = load(mass_hbm, mass_ref, 7)
    load_pick = load(pick_hbm, pick_ref, 8)
    load_remap = load(remap_hbm, remap_ref, 9)
    load_place = load(place_hbm, place_ref, 10)
    for copy in (*load_rows, load_high, load_low, load_winds, load_mass):
        copy.wait()

    def tracer_row(a):
        return tracers_ref[a].reshape(2 * levels, across)

    derivative = gll_matrix()

    def weigh(a):
        here = tracer_row(a)
        high, low = split(here)
        along_y = dot(high, dhigh_ref[...]) + dot(low, dhigh_ref[...]) + dot(high, dlow_ref[...])
        along_x = sum(float(derivative[a, c]) * tracer_row(c) for c in range(4))
        first = winds_ref[0, :, a, :].astype(jnp.float32)
        second = winds_ref[1, :, a, :].astype(jnp.float32)
        mass = mass_ref[a : a + 1, :]
        first, second = first * mass, second * mass
        for k in range(2):
            part = slice(k * levels, (k + 1) * levels)
            weighted[a, part, :] = -(first * along_x[part] + second * along_y[part])

    for a in (0, 3):
        weigh(a)
    rows_out[0] = weighted[3].astype(jnp.bfloat16)
    rows_out[1] = weighted[0].astype(jnp.bfloat16)

    pl.semaphore_wait(barrier, 8)
    copies = []

    def send(src, dst, slot, i):
        copy = pltpu.make_async_remote_copy(
            src_ref=src, dst_ref=dst, send_sem=send_sem.at[slot], recv_sem=recv_sem.at[slot],
            device_id=peer(i), device_id_type=MESH,
        )
        copy.start()
        copies.append(copy)
        return copy

    row_copies = [send(rows_out.at[i], rows_in.at[i], i, i) for i in range(2)]
    mass_copies = [send(mass_ref, mass_in.at[i], 2 + i, i) for i in range(8)]

    for a in (1, 2):
        weigh(a)
    load_pick.wait()
    ends = None
    for a in range(4):
        term = lax.dot_general(
            pick_ref[a], weighted[a].astype(jnp.bfloat16), (((1,), (1,)), ((), ())),
            preferred_element_type=jnp.float32,
        )
        ends = term if ends is None else ends + term
    ends_out[...] = ends
    end_copies = [send(ends_out, ends_in.at[i - 2], 8 + i, i) for i in range(2, 8)]

    lane = lax.broadcasted_iota(jnp.int32, (1, across), 1)
    takes_before = (lane % 4 == 0) & (lane > 0)
    takes_after = (lane % 4 == 3) & (lane < across - 1)

    half = across // 2
    load_remap.wait()

    def store_cells(mixed, first, p):
        high, low = split(mixed)
        cells = (dot(high, remap_ref[...]) + dot(low, remap_ref[...])) * (1.0 / 400.0)
        count = cells.shape[0]
        start_ref[p * half : (p + 1) * half, first : first + count] = cells.T.astype(jnp.bfloat16)

    for p in range(2):
        parts = [
            sum(
                remap_ints[p][a] * winds_ref[k, :, a, :].astype(jnp.float32)
                for a in range(4) if remap_ints[p][a]
            )
            for k in range(2)
        ]
        store_cells(jnp.concatenate(parts, axis=0), 2 * levels, p)

    for copy in mass_copies:
        copy.wait_recv()

    def join_rows(middle, upper, lower):
        return [middle[0:1] + upper[3:4], middle[1:2], middle[2:3], middle[3:4] + lower[0:1]]

    own = join_rows(mass_ref, mass_in[FROM_UP], mass_in[FROM_DOWN])
    left = join_rows(mass_in[FROM_LEFT], mass_in[FROM_UL], mass_in[FROM_DL])
    right = join_rows(mass_in[FROM_RIGHT], mass_in[FROM_UR], mass_in[FROM_DR])
    scales = []
    for a in range(4):
        before = pltpu.roll(jnp.where(lane == across - 1, left[a], own[a]), 1, 1)
        after = pltpu.roll(jnp.where(lane == 0, right[a], own[a]), across - 1, 1)
        total = own[a] + jnp.where(lane % 4 == 0, before, 0.0) + jnp.where(lane % 4 == 3, after, 0.0)
        scales.append(time_step / total)

    load_place.wait()
    for copy in row_copies:
        copy.wait_recv()
    for copy in end_copies:
        copy.wait_recv()

    received = ends_in[...].reshape(48, ends_in.shape[-1]).astype(jnp.bfloat16)
    received = received.astype(jnp.float32).T.astype(jnp.bfloat16)
    mixed = [None, None]
    stores = []
    for a in range(4):
        value = weighted[a]
        if a == 0:
            value = value + rows_in[FROM_UP].astype(jnp.float32)
        if a == 3:
            value = value + rows_in[FROM_DOWN].astype(jnp.float32)
        before = pltpu.roll(value, 1, 1)
        after = pltpu.roll(value, across - 1, 1)
        total = value + jnp.where(takes_before, before, jnp.where(takes_after, after, 0.0))
        total = total + dot(received, place_ref[a])
        updated = tracer_row(a) + scales[a] * total
        next_ref[a] = updated.reshape(2, levels, across)
        store = pltpu.make_async_copy(next_ref.at[a], next_hbm.at[a], store_sem.at[a])
        store.start()
        stores.append(store)
        for p in range(2):
            if remap_ints[p][a]:
                term = remap_ints[p][a] * updated
                mixed[p] = term if mixed[p] is None else mixed[p] + term
    for p in range(2):
        store_cells(mixed[p], 0, p)

    for copy in stores:
        copy.wait()
    for copy in copies:
        copy.wait_send()


def columns_kernel(
    rows_hbm, start_ref, cost_ref, win_ref, wout_ref, next_hbm, cols_ref, rows_ref, load_sem, store_sem
):
    loads = [
        pltpu.make_async_copy(rows_hbm.at[a], rows_ref.at[a], load_sem.at[a]) for a in range(4)
    ]
    stores = [
        pltpu.make_async_copy(rows_ref.at[a], next_hbm.at[:, :, a, :], store_sem.at[a])
        for a in range(4)
    ]
    for copy in loads:
        copy.start()
    features, hidden_size = win_ref.shape
    half = cost_ref.shape[1]
    cost = jnp.concatenate(
        [
            jnp.broadcast_to(cost_ref[p : p + 1, :].astype(jnp.float32), (half, half)).T
            for p in range(2)
        ],
        axis=0,
    )
    cost = jnp.concatenate([cost] * (features // half), axis=1)
    chunk = hidden_size // 4
    current = start_ref[...].astype(jnp.float32)
    for step in range(3):
        inputs = current.astype(jnp.bfloat16)
        change = None
        for c in range(4):
            part = slice(c * chunk, (c + 1) * chunk)
            hidden = jax.nn.gelu(dot(inputs, win_ref[:, part])).astype(jnp.bfloat16)
            term = dot(hidden, wout_ref[part, :])
            change = term if change is None else change + term
        current = current + jnp.where(cost > step + 0.5, change, 0.0)
        if step == 0:
            for load, store in zip(loads, stores):
                load.wait()
                store.start()
    cols_ref[...] = jnp.stack([current[:half].T, current[half:].T], axis=1).astype(jnp.bfloat16)
    for copy in stores:
        copy.wait()


def shards(sizes, tracers, winds, node_mass, column_cost, weight_in, weight_out):
    levels, extent, across = tracers.shape[1:]
    features, hidden = weight_in.shape
    channels = 2 * levels
    vmem = pl.BlockSpec(memory_space=pltpu.VMEM)
    hbm = pl.BlockSpec(memory_space=pltpu.HBM)
    f32, bf16 = jnp.float32, jnp.bfloat16
    rows = (extent, 2, levels, across)
    tables = constants(across)
    columns = column_cost.size
    next_rows, start = pl.pallas_call(
        functools.partial(kernel, sizes),
        out_shape=(
            jax.ShapeDtypeStruct(rows, f32),
            jax.ShapeDtypeStruct((columns, features), bf16),
        ),
        in_specs=[hbm] * 8,
        out_specs=(hbm, vmem),
        scratch_shapes=[
            pltpu.VMEM(rows, f32),
            pltpu.VMEM(winds.shape, bf16),
            pltpu.VMEM(node_mass.shape, f32),
            *[pltpu.VMEM(table.shape, bf16) for table in tables],
            pltpu.VMEM((extent, channels, across), f32),
            pltpu.VMEM(rows, f32),
            pltpu.VMEM((2, channels, across), bf16),
            pltpu.VMEM((2, channels, across), bf16),
            pltpu.VMEM((8, channels), f32),
            pltpu.VMEM((6, 8, channels), f32),
            pltpu.VMEM((8, extent, across), f32),
            pltpu.SemaphoreType.DMA((11,)),
            pltpu.SemaphoreType.DMA((4,)),
            pltpu.SemaphoreType.DMA((16,)),
            pltpu.SemaphoreType.DMA((16,)),
        ],
        compiler_params=pltpu.CompilerParams(
            collective_id=0, has_side_effects=True
        ),
        cost_estimate=pl.CostEstimate(
            flops=10**9, bytes_accessed=4 * 2**20, transcendentals=0
        ),
    )(tracers, winds, node_mass, *tables)
    tracers_next, cols = pl.pallas_call(
        columns_kernel,
        out_shape=(
            jax.ShapeDtypeStruct(tracers.shape, f32),
            jax.ShapeDtypeStruct((features, 2, across // 2), bf16),
        ),
        in_specs=[hbm] + [vmem] * 4,
        out_specs=(hbm, vmem),
        scratch_shapes=[
            pltpu.VMEM(rows, f32),
            pltpu.SemaphoreType.DMA((4,)),
            pltpu.SemaphoreType.DMA((4,)),
        ],

    )(next_rows, start, column_cost, weight_in, weight_out)
    return tracers_next, cols.reshape(4, levels, 2, across // 2)


def solution(mesh):
    grid = P(None, None, "grp", "bal")
    flat = P("grp", "bal")
    sizes = (mesh.shape["grp"], mesh.shape["bal"])
    return jax.shard_map(
        functools.partial(shards, sizes),
        mesh=mesh,
        in_specs=(grid, grid, flat, flat, P(), P()),
        out_specs=(grid, grid),
        check_vma=False,
    )
```

profile of v0, /device:TPU:0, one launch (start us, length us, event | category | flops | bytes accessed | tf_op | source)
XLA Modules:
  0.0 17.8 jit_solution(2516880146567551623)
XLA Ops:
  0.6 12.6 %shard_map.122 = (f32[4,2,64,256]{3,2,1,0:T(8,128)}, bf16[256,256]{1,0:T(8,128)(2,1)}) custom-call(f32[2,64,4,256]{3,2,1,0:T(4,128)} %tracers_hbm.1, bf16[2,64,4,256]{3,2,1,0:T(4,128)(2,1)} %winds_hbm.1, f32[4,256]{1,0:T(4,128)} %mass_hbm.1, bf16[256,256]{1,0:T(8,128)(2,1)} %constant.10.clone.dhigh_hbm, bf16[256,256]{1,0:T(8,128)(2,1)} %constant.11.clone.dlow_hbm, ...), custom_call_target="tpu_custom_call" | custom-call | flops 1000000000 | bytes 4194304 | tf_op jit(solution)/shard_map/pallas_call | solution.py:290
  13.2 4.6 %shard_map.123 = (f32[2,64,4,256]{3,2,1,0:T(4,128)}, bf16[256,2,128]{2,1,0:T(2,128)(2,1)}) custom-call(f32[4,2,64,256]{3,2,1,0:T(8,128)} %get-tuple-element.6.rows_hbm, bf16[256,256]{1,0:T(8,128)(2,1)} %get-tuple-element.7.start_ref, s32[2,128]{1,0:T(2,128)} %cost_ref.1, bf16[256,1024]{1,0:T(8,128)(2,1)} %win_ref.1, bf16[1024,256]{1,0:T(8,128)(2,1)} %wout_ref.1), custom_call_target="tpu_custom_call" | custom-call | tf_op jit(solution)/shard_map/pallas_call | solution.py:322
where the time goes:
time: 18 us; the launch traced here: 17.8 us
  Pallas kernels  17.1 us (95%)
  between operations  0.64 us (4%)
    pallas_call x1, Pallas kernels, shards(): pl.pallas_call(functools.partial(kernel, sizes), out_shape=(jax.ShapeDtyp...  12.6 us
    pallas_call x1, Pallas kernels, shards(): pl.pallas_call(columns_kernel, out_shape=(jax.ShapeDtypeStruct(tracers.sh...  4.57 us

commit v1 on v0

v1 whole, which is shorter than its diff:
```python
import functools

import jax
import jax.numpy as jnp
import numpy as np
from jax import lax
from jax.experimental import pallas as pl
from jax.experimental.pallas import tpu as pltpu
from jax.sharding import PartitionSpec as P

MESH = pl.DeviceIdType.MESH
time_step = 0.02
remap_ints = ((9.0, 8.0, 3.0, 0.0), (0.0, 3.0, 8.0, 9.0))
gll_points = (-1.0, -0.4472135954999579, 0.4472135954999579, 1.0)

DIRS = ((1, 0), (-1, 0), (0, 1), (0, -1), (1, 1), (1, -1), (-1, 1), (-1, -1))
FROM_UP, FROM_DOWN, FROM_LEFT, FROM_RIGHT = 0, 1, 2, 3
FROM_UL, FROM_UR, FROM_DL, FROM_DR = 4, 5, 6, 7


def gll_matrix():
    points = gll_points
    matrix = np.zeros((4, 4))
    for i in range(4):
        for j in range(4):
            if i == j:
                matrix[i, i] = 2.0 * sum(
                    1.0 / (points[i] - points[k]) for k in range(4) if k != i
                )
            else:
                num = den = 1.0
                for k in range(4):
                    if k != i:
                        num *= points[i] - points[k]
                    if k != j:
                        den *= points[j] - points[k]
                matrix[i, j] = 2.0 * num / (den * (points[i] - points[j]))
    return matrix


def constants(across):
    elements, half = across // 4, across // 2
    eye = np.eye(elements)
    along = np.kron(eye, gll_matrix().T).astype(np.float32)
    high = along.astype(jnp.bfloat16)
    low = (along - high.astype(np.float32)).astype(jnp.bfloat16)
    remap = np.kron(eye, np.array(remap_ints).T).astype(jnp.bfloat16)
    pick = np.zeros((4, 8, across), np.float32)
    place = np.zeros((16, 5 * across), np.float32)
    for a in range(4):
        pick[a, a, 0] = 1.0
        pick[a, 4 + a, across - 1] = 1.0
        for part in range(2):
            place[8 * part + a, a * across] = 1.0
            place[8 * part + 4 + a, a * across + across - 1] = 1.0
            for p in range(2):
                first = 4 * across + p * half
                place[8 * part + a, first] = remap_ints[p][a] * remap_ints[0][0]
                place[8 * part + 4 + a, first + half - 1] = remap_ints[p][a] * remap_ints[1][3]
    return high, low, remap, pick.astype(jnp.bfloat16), place.astype(jnp.bfloat16)


def dot(a, b):
    return jnp.dot(a, b, preferred_element_type=jnp.float32)


def split(value):
    high = value.astype(jnp.bfloat16)
    return high, (value - high.astype(jnp.float32)).astype(jnp.bfloat16)


def kernel(
    sizes,
    tracers_hbm, winds_hbm, mass_hbm,
    dhigh_hbm, dlow_hbm, remap_hbm, pick_hbm, place_hbm, win_hbm, wout_hbm,
    next_ref, start_ref, win_t_ref, wout_t_ref,
    tracers_ref, winds_ref, mass_ref,
    dhigh_ref, dlow_ref, remap_ref, pick_ref, place_ref, win_ref, wout_ref,
    weighted, cells_ref, rows_out, rows_in, corners_out, ends_out, ends_in,
    mass_in, local_sem, send_sem, recv_sem, ack_sem,
):
    n_grp, n_bal = sizes
    levels, across = winds_ref.shape[1], winds_ref.shape[3]
    grp, bal = lax.axis_index("grp"), lax.axis_index("bal")
    is_first, is_last = bal == 0, bal == n_bal - 1

    def peer(i):
        dg, db = DIRS[i]
        return (lax.rem(grp + dg + n_grp, n_grp), lax.rem(bal + db + n_bal, n_bal))

    to_left = [i for i in range(8) if DIRS[i][1] == -1]
    to_right = [i for i in range(8) if DIRS[i][1] == 1]

    barrier = pltpu.get_barrier_semaphore()

    def greet(i):
        pl.semaphore_signal(barrier, inc=1, device_id=peer(i), device_id_type=MESH)

    for i in range(2):
        greet(i)

    @pl.when(is_first)
    def _():
        for i in to_left:
            greet(i)

    @pl.when(jnp.logical_not(is_last))
    def _():
        for i in to_right:
            greet(i)

    def load(src, dst, slot):
        copy = pltpu.make_async_copy(src, dst, local_sem.at[slot])
        copy.start()
        return copy

    load_mass = load(mass_hbm, mass_ref, 7)
    load_rows = [load(tracers_hbm.at[:, :, a, :], tracers_ref.at[a], a) for a in range(4)]
    load_winds = load(winds_hbm, winds_ref, 6)
    load_high = load(dhigh_hbm, dhigh_ref, 4)
    load_low = load(dlow_hbm, dlow_ref, 5)
    load_pick = load(pick_hbm, pick_ref, 8)
    load_remap = load(remap_hbm, remap_ref, 9)
    load_place = load(place_hbm, place_ref, 10)

    load_mass.wait()
    mass_ends = jnp.concatenate(
        [
            jnp.broadcast_to(mass_ref[a : a + 1, lane : lane + 1], (1, 2 * levels))
            for lane in (0, across - 1) for a in range(4)
        ],
        axis=0,
    )
    corners_out[8:16, :] = mass_ends
    ends_out[8:16, :] = mass_ends
    for copy in (load_high, load_low, load_winds, *load_rows):
        copy.wait()

    def tracer_row(a):
        return tracers_ref[a].reshape(2 * levels, across)

    derivative = gll_matrix()

    def weigh(a):
        here = tracer_row(a)
        high, low = split(here)
        along_y = dot(high, dhigh_ref[...]) + dot(low, dhigh_ref[...]) + dot(high, dlow_ref[...])
        along_x = sum(float(derivative[a, c]) * tracer_row(c) for c in range(4))
        first = winds_ref[0, :, a, :].astype(jnp.float32)
        second = winds_ref[1, :, a, :].astype(jnp.float32)
        mass = mass_ref[a : a + 1, :]
        first, second = first * mass, second * mass
        for k in range(2):
            part = slice(k * levels, (k + 1) * levels)
            weighted[a, part, :] = -(first * along_x[part] + second * along_y[part])

    def picked(a):
        return lax.dot_general(
            pick_ref[a], weighted[a].astype(jnp.bfloat16), (((1,), (1,)), ((), ())),
            preferred_element_type=jnp.float32,
        )

    for a in (0, 3):
        weigh(a)
    rows_out[0] = weighted[3].astype(jnp.bfloat16)
    rows_out[1] = weighted[0].astype(jnp.bfloat16)
    load_pick.wait()
    corners = picked(0) + picked(3)
    corners_out[0:8, :] = corners

    def remote(src, dst, slot, i):
        return pltpu.make_async_remote_copy(
            src_ref=src, dst_ref=dst, send_sem=send_sem.at[slot], recv_sem=recv_sem.at[slot],
            device_id=peer(i), device_id_type=MESH,
        )

    mass_copies = [remote(mass_ref, mass_in.at[i], i, i) for i in range(2)]
    row_copies = [remote(rows_out.at[i], rows_in.at[i], 2 + i, i) for i in range(2)]
    end_copies = [
        remote(ends_out if i in (2, 3) else corners_out, ends_in.at[i], 4 + i, i) for i in range(8)
    ]

    before = jnp.where(bal > 0, 3, 0) + jnp.where(is_last, 3, 0)
    pl.semaphore_wait(barrier, 2 + before)

    def answer(slot, i):
        pl.semaphore_signal(ack_sem.at[slot], inc=1, device_id=peer(i), device_id_type=MESH)

    @pl.when(jnp.logical_not(is_first))
    def _():
        for i in to_left:
            answer(1, i)
        for i in to_left:
            if i > 3:
                end_copies[i].start()

    @pl.when(is_last)
    def _():
        for i in to_right:
            answer(0, i)
        for i in to_right:
            if i > 3:
                end_copies[i].start()

    for copy in (*mass_copies, *row_copies, *end_copies[:2]):
        copy.start()

    for a in (1, 2):
        weigh(a)
    ends_out[0:8, :] = corners + (picked(1) + picked(2))

    @pl.when(jnp.logical_not(is_first))
    def _():
        end_copies[3].start()

    @pl.when(is_last)
    def _():
        end_copies[2].start()

    @pl.when(jnp.logical_not(is_last))
    def _():
        pl.semaphore_wait(ack_sem.at[1], 3)
        for i in to_right:
            end_copies[i].start()

    load_win = load(win_hbm, win_ref, 11)
    load_wout = load(wout_hbm, wout_ref, 12)

    lane = lax.broadcasted_iota(jnp.int32, (1, across), 1)
    takes_before = (lane % 4 == 0) & (lane > 0)
    takes_after = (lane % 4 == 3) & (lane < across - 1)
    inside = (lane > 0) & (lane < across - 1)

    half = across // 2
    load_remap.wait()

    def cells(mixed):
        high, low = split(mixed)
        return dot(high, remap_ref[...]) + dot(low, remap_ref[...])

    for p in range(2):
        parts = [
            sum(
                remap_ints[p][a] * winds_ref[k, :, a, :].astype(jnp.float32)
                for a in range(4) if remap_ints[p][a]
            )
            for k in range(2)
        ]
        start_ref[2 * levels :, p * half : (p + 1) * half] = (
            cells(jnp.concatenate(parts, axis=0)) * (1.0 / 400.0)
        ).astype(jnp.bfloat16)

    load_win.wait()
    win_t_ref[...] = win_ref[...].T
    load_wout.wait()
    wout_t_ref[...] = wout_ref[...].T

    for copy in mass_copies:
        copy.wait_recv()
    own = [mass_ref[a : a + 1, :] for a in range(4)]
    own[0] = own[0] + mass_in[FROM_UP, 3:4, :]
    own[3] = own[3] + mass_in[FROM_DOWN, 0:1, :]

    def joined(value):
        earlier = pltpu.roll(value, 1, 1)
        later = pltpu.roll(value, across - 1, 1)
        return value + jnp.where(takes_before, earlier, jnp.where(takes_after, later, 0.0))

    scales = [jnp.where(inside, time_step / joined(own[a]), 0.0) for a in range(4)]

    load_place.wait()

    @pl.when(is_first)
    def _():
        pl.semaphore_wait(ack_sem.at[0], 3)
        for i in to_left:
            end_copies[i].start()

    for copy in row_copies:
        copy.wait_recv()
    mixed = [None, None]
    for a in range(4):
        value = weighted[a]
        if a == 0:
            value = value + rows_in[FROM_UP].astype(jnp.float32)
        if a == 3:
            value = value + rows_in[FROM_DOWN].astype(jnp.float32)
        updated = tracer_row(a) + scales[a] * joined(value)
        next_ref[a] = updated
        for p in range(2):
            if remap_ints[p][a]:
                term = remap_ints[p][a] * updated
                mixed[p] = term if mixed[p] is None else mixed[p] + term
    for p in range(2):
        cells_ref[:, p * half : (p + 1) * half] = cells(mixed[p])

    for copy in end_copies:
        copy.wait_recv()

    def assembled(mine, first):
        def row(i, r):
            return ends_in[i, first + r : first + r + 1, :]

        lines = []
        for side, lateral, upper, lower in (
            (0, FROM_LEFT, FROM_UL, FROM_DL), (1, FROM_RIGHT, FROM_UR, FROM_DR)
        ):
            near, far = 4 * side, 4 - 4 * side
            for a in range(4):
                line = mine[near + a : near + a + 1, :] + row(lateral, far + a)
                if a == 0:
                    line = line + (row(FROM_UP, near + 3) + row(upper, far + 3))
                if a == 3:
                    line = line + (row(FROM_DOWN, near) + row(lower, far))
                lines.append(line)
        return jnp.concatenate(lines, axis=0)

    change = assembled(ends_out[0:8, :], 0) * (time_step / assembled(ends_out[8:16, :], 8))
    high = change.astype(jnp.bfloat16).astype(jnp.float32)
    parts = jnp.concatenate([high, change - high], axis=0).T.astype(jnp.bfloat16)
    final = cells_ref[...] + dot(parts, place_ref[:, 4 * across :])
    start_ref[0 : 2 * levels, :] = (final * (1.0 / 400.0)).astype(jnp.bfloat16)
    for a in range(4):
        next_ref[a] = next_ref[a] + dot(parts, place_ref[:, a * across : (a + 1) * across])

    for copy in (*mass_copies, *row_copies, *end_copies):
        copy.wait_send()


def doubled_gelu(value):
    inner = value * (0.7978845608028654 + 0.035677408136300125 * (value * value))
    return value + value * jnp.tanh(inner)


def columns_kernel(
    rows_ref, start_ref, cost_hbm, win_ref, wout_ref, next_hbm, cols_ref, cost_ref, load_sem, store_sem
):
    load_cost = pltpu.make_async_copy(cost_hbm, cost_ref, load_sem)
    load_cost.start()
    levels = next_hbm.shape[1]
    stores = [
        pltpu.make_async_copy(
            rows_ref.at[a, pl.ds(k * levels, levels), :], next_hbm.at[k, :, a, :], store_sem.at[a, k]
        )
        for a in range(4) for k in range(2)
    ]
    for copy in stores:
        copy.start()
    hidden_size, features = win_ref.shape
    half = cost_ref.shape[1]
    chunk = hidden_size // 4
    current = start_ref[...].astype(jnp.float32)
    for step in range(3):
        inputs = current.astype(jnp.bfloat16)
        change = None
        for c in range(4):
            part = slice(c * chunk, (c + 1) * chunk)
            hidden = doubled_gelu(dot(win_ref[part, :], inputs)).astype(jnp.bfloat16)
            term = dot(wout_ref[:, part], hidden)
            change = term if change is None else change + term
        if step == 0:
            load_cost.wait()
            cost = jnp.concatenate([cost_ref[0:1, :], cost_ref[1:2, :]], axis=1)
        current = current + jnp.where(cost > step, 0.5, 0.0) * change
    cols_ref[...] = jnp.stack([current[:, :half], current[:, half:]], axis=1).astype(jnp.bfloat16)
    for copy in stores:
        copy.wait()


def shards(sizes, tracers, winds, node_mass, column_cost, weight_in, weight_out):
    levels, extent, across = tracers.shape[1:]
    features, hidden = weight_in.shape
    channels = 2 * levels
    vmem = pl.BlockSpec(memory_space=pltpu.VMEM)
    hbm = pl.BlockSpec(memory_space=pltpu.HBM)
    f32, bf16 = jnp.float32, jnp.bfloat16
    rows = (extent, channels, across)
    tables = constants(across)
    columns = column_cost.size
    operands = (tracers, winds, node_mass, *map(jnp.asarray, tables), weight_in, weight_out)
    next_rows, start, win_t, wout_t = pl.pallas_call(
        functools.partial(kernel, sizes),
        out_shape=(
            jax.ShapeDtypeStruct(rows, f32),
            jax.ShapeDtypeStruct((features, columns), bf16),
            jax.ShapeDtypeStruct((hidden, features), bf16),
            jax.ShapeDtypeStruct((features, hidden), bf16),
        ),
        in_specs=[hbm] * 10,
        out_specs=(vmem,) * 4,
        scratch_shapes=[
            pltpu.VMEM((extent, 2, levels, across), f32),
            pltpu.VMEM(winds.shape, bf16),
            pltpu.VMEM(node_mass.shape, f32),
            *[pltpu.VMEM(table.shape, bf16) for table in tables],
            pltpu.VMEM(weight_in.shape, bf16),
            pltpu.VMEM(weight_out.shape, bf16),
            pltpu.VMEM(rows, f32),
            pltpu.VMEM((channels, across), f32),
            pltpu.VMEM((2, channels, across), bf16),
            pltpu.VMEM((2, channels, across), bf16),
            pltpu.VMEM((16, channels), f32),
            pltpu.VMEM((16, channels), f32),
            pltpu.VMEM((8, 16, channels), f32),
            pltpu.VMEM((2, extent, across), f32),
            pltpu.SemaphoreType.DMA((13,)),
            pltpu.SemaphoreType.DMA((12,)),
            pltpu.SemaphoreType.DMA((12,)),
            pltpu.SemaphoreType.REGULAR((2,)),
        ],
        compiler_params=pltpu.CompilerParams(
            collective_id=0, has_side_effects=True, vmem_limit_bytes=24 * 2**20
        ),
        cost_estimate=pl.CostEstimate(
            flops=10**9, bytes_accessed=4 * 2**20, transcendentals=0
        ),
    )(*(pltpu.with_memory_space_constraint(x, pltpu.HBM) for x in operands))
    tracers_next, cols = pl.pallas_call(
        columns_kernel,
        out_shape=(
            jax.ShapeDtypeStruct(tracers.shape, f32),
            jax.ShapeDtypeStruct((features, 2, across // 2), bf16),
        ),
        in_specs=[vmem, vmem, hbm, vmem, vmem],
        out_specs=(hbm, vmem),
        scratch_shapes=[
            pltpu.VMEM(column_cost.shape, column_cost.dtype),
            pltpu.SemaphoreType.DMA,
            pltpu.SemaphoreType.DMA((4, 2)),
        ],
        compiler_params=pltpu.CompilerParams(vmem_limit_bytes=24 * 2**20),
    )(next_rows, start, pltpu.with_memory_space_constraint(column_cost, pltpu.HBM), win_t, wout_t)
    return tracers_next, cols.reshape(4, levels, 2, across // 2)


def solution(mesh):
    grid = P(None, None, "grp", "bal")
    flat = P("grp", "bal")
    sizes = (mesh.shape["grp"], mesh.shape["bal"])
    return jax.shard_map(
        functools.partial(shards, sizes),
        mesh=mesh,
        in_specs=(grid, grid, flat, flat, P(), P()),
        out_specs=(grid, grid),
        check_vma=False,
    )
```

time: 18 us -> 14.9 us (0.83)
  Pallas kernels: 17.1 us -> 14.1 us
    pallas_call x1, Pallas kernels: 4.57 us -> 3.02 us  [shards(): pl.pallas_call(columns_kernel, out_shape=(jax.ShapeDtypeStruct(tracers.sh...]
    pallas_call x1, Pallas kernels: 12.6 us -> 11.1 us  [shards(): pl.pallas_call(functools.partial(kernel, sizes), out_shape=(jax.ShapeDtyp...]
where the time goes in v1:
time: 14.9 us; the launch traced here: 14.7 us
  Pallas kernels  14.1 us (95%)
  between operations  0.64 us (4%)
    pallas_call x1, Pallas kernels, shards(): pl.pallas_call(functools.partial(kernel, sizes), out_shape=(jax.ShapeDtyp...  11.1 us
    pallas_call x1, Pallas kernels, shards(): pl.pallas_call(columns_kernel, out_shape=(jax.ShapeDtypeStruct(tracers.sh...  3.02 us

profile of v1, /device:TPU:0, one launch (start us, length us, event | category | flops | bytes accessed | tf_op | source)
XLA Modules:
  0.0 14.7 jit_solution(10163047752408637851)
XLA Ops:
  0.6 11.1 %shard_map.122 = (f32[4,128,256]{2,1,0:T(8,128)S(1)}, bf16[256,256]{1,0:T(8,128)(2,1)S(1)}, bf16[1024,256]{1,0:T(8,128)(2,1)S(1)}, bf16[256,1024]{1,0:T(8,128)(2,1)S(1)}) custom-call(f32[2,64,4,256]{3,2,1,0:T(4,128)} %tracers_hbm.1, bf16[2,64,4,256]{3,2,1,0:T(4,128)(2,1)} %winds_hbm.1, f32[4,256]{1,0:T(4,128)} %mass_hbm.1, ...), custom_call_target="tpu_custom_call" | custom-call | flops 1000000000 | bytes 4194304 | tf_op jit(solution)/shard_map/pallas_call | solution.py:381
  11.7 3.0 %shard_map.123 = (f32[2,64,4,256]{3,2,1,0:T(4,128)}, bf16[256,2,128]{2,1,0:T(2,128)(2,1)}) custom-call(f32[4,128,256]{2,1,0:T(8,128)S(1)} %get-tuple-element.8.rows_ref, bf16[256,256]{1,0:T(8,128)(2,1)S(1)} %get-tuple-element.9.start_ref, s32[2,128]{1,0:T(2,128)} %cost_hbm.1, bf16[1024,256]{1,0:T(8,128)(2,1)S(1)} %get-tuple-element.10.win_ref, ...), custom_call_target="tpu_custom_call" | custom-call | tf_op jit(solution)/shard_map/pallas_call | solution.py:418

commit v2 on v1

--- a/solution.py
+++ b/solution.py
@@ -72,12 +72,12 @@
 def kernel(
     sizes,
     tracers_hbm, winds_hbm, mass_hbm,
-    dhigh_hbm, dlow_hbm, remap_hbm, pick_hbm, place_hbm, win_hbm, wout_hbm,
-    next_ref, start_ref, win_t_ref, wout_t_ref,
+    dhigh_hbm, dlow_hbm, remap_hbm, pick_hbm, place_hbm, win_hbm, wout_hbm, cost_hbm,
+    next_ref, start_ref, win_t_ref, wout_t_ref, cost_out_ref,
     tracers_ref, winds_ref, mass_ref,
-    dhigh_ref, dlow_ref, remap_ref, pick_ref, place_ref, win_ref, wout_ref,
-    weighted, cells_ref, rows_out, rows_in, corners_out, ends_out, ends_in,
-    mass_in, local_sem, send_sem, recv_sem, ack_sem,
+    dhigh_ref, dlow_ref, remap_ref, pick_ref, place_ref, win_ref, wout_ref, cost_ref,
+    weighted, cells_ref, rows_out, rows_in, corners_out, corners_in, sides_out, sides_in,
+    mass_out, mass_in, local_sem, send_sem, recv_sem, ack_sem,
 ):
     n_grp, n_bal = sizes
     levels, across = winds_ref.shape[1], winds_ref.shape[3]
@@ -90,24 +90,6 @@
 
     to_left = [i for i in range(8) if DIRS[i][1] == -1]
     to_right = [i for i in range(8) if DIRS[i][1] == 1]
-
-    barrier = pltpu.get_barrier_semaphore()
-
-    def greet(i):
-        pl.semaphore_signal(barrier, inc=1, device_id=peer(i), device_id_type=MESH)
-
-    for i in range(2):
-        greet(i)
-
-    @pl.when(is_first)
-    def _():
-        for i in to_left:
-            greet(i)
-
-    @pl.when(jnp.logical_not(is_last))
-    def _():
-        for i in to_right:
-            greet(i)
 
     def load(src, dst, slot):
         copy = pltpu.make_async_copy(src, dst, local_sem.at[slot])
@@ -123,16 +105,38 @@
     load_remap = load(remap_hbm, remap_ref, 9)
     load_place = load(place_hbm, place_ref, 10)
 
+    barrier = pltpu.get_barrier_semaphore()
+
+    def greet(i):
+        pl.semaphore_signal(barrier, inc=1, device_id=peer(i), device_id_type=MESH)
+
+    for i in range(2):
+        greet(i)
+
+    @pl.when(is_first)
+    def _():
+        for i in to_left:
+            greet(i)
+
+    @pl.when(jnp.logical_not(is_last))
+    def _():
+        for i in to_right:
+            greet(i)
+
     load_mass.wait()
-    mass_ends = jnp.concatenate(
-        [
-            jnp.broadcast_to(mass_ref[a : a + 1, lane : lane + 1], (1, 2 * levels))
+
+    def outermost(rows):
+        return [
+            jnp.broadcast_to(rows[a][:, lane : lane + 1], (1, 2 * levels))
             for lane in (0, across - 1) for a in range(4)
-        ],
-        axis=0,
-    )
-    corners_out[8:16, :] = mass_ends
-    ends_out[8:16, :] = mass_ends
+        ]
+
+    own = [mass_ref[a : a + 1, :] for a in range(4)]
+    mass_out[0] = own[3]
+    mass_out[1] = own[0]
+    mass_ends = outermost(own)
+    for side in range(2):
+        sides_out[side, 4:8, :] = jnp.concatenate(mass_ends[4 * side : 4 * side + 4], axis=0)
     for copy in (load_high, load_low, load_winds, *load_rows):
         copy.wait()
 
@@ -154,11 +158,13 @@
             part = slice(k * levels, (k + 1) * levels)
             weighted[a, part, :] = -(first * along_x[part] + second * along_y[part])
 
+    def picks(a, value):
+        return lax.dot_general(
+            pick_ref[a], value, (((1,), (1,)), ((), ())), preferred_element_type=jnp.float32
+        )
+
     def picked(a):
-        return lax.dot_general(
-            pick_ref[a], weighted[a].astype(jnp.bfloat16), (((1,), (1,)), ((), ())),
-            preferred_element_type=jnp.float32,
-        )
+        return picks(a, weighted[a].astype(jnp.bfloat16))
 
     for a in (0, 3):
         weigh(a)
@@ -166,7 +172,8 @@
     rows_out[1] = weighted[0].astype(jnp.bfloat16)
     load_pick.wait()
     corners = picked(0) + picked(3)
-    corners_out[0:8, :] = corners
+    for c, line in enumerate((7, 3, 4, 0)):
+        corners_out[c] = jnp.concatenate([corners[line : line + 1, :], mass_ends[line]], axis=0)
 
     def remote(src, dst, slot, i):
         return pltpu.make_async_remote_copy(
@@ -174,11 +181,13 @@
             device_id=peer(i), device_id_type=MESH,
         )
 
-    mass_copies = [remote(mass_ref, mass_in.at[i], i, i) for i in range(2)]
+    mass_copies = [remote(mass_out.at[i], mass_in.at[i], i, i) for i in range(2)]
     row_copies = [remote(rows_out.at[i], rows_in.at[i], 2 + i, i) for i in range(2)]
-    end_copies = [
-        remote(ends_out if i in (2, 3) else corners_out, ends_in.at[i], 4 + i, i) for i in range(8)
-    ]
+    end_copies = {
+        2: remote(sides_out.at[1], sides_in.at[0], 4, 2),
+        3: remote(sides_out.at[0], sides_in.at[1], 5, 3),
+        **{4 + c: remote(corners_out.at[c], corners_in.at[c], 6 + c, 4 + c) for c in range(4)},
+    }
 
     before = jnp.where(bal > 0, 3, 0) + jnp.where(is_last, 3, 0)
     pl.semaphore_wait(barrier, 2 + before)
@@ -186,28 +195,30 @@
     def answer(slot, i):
         pl.semaphore_signal(ack_sem.at[slot], inc=1, device_id=peer(i), device_id_type=MESH)
 
+    @pl.when(is_last)
+    def _():
+        for i in to_right:
+            if i > 3:
+                end_copies[i].start()
+        for i in to_right:
+            answer(0, i)
+
     @pl.when(jnp.logical_not(is_first))
     def _():
-        for i in to_left:
-            answer(1, i)
         for i in to_left:
             if i > 3:
                 end_copies[i].start()
-
-    @pl.when(is_last)
-    def _():
-        for i in to_right:
-            answer(0, i)
-        for i in to_right:
-            if i > 3:
-                end_copies[i].start()
-
-    for copy in (*mass_copies, *row_copies, *end_copies[:2]):
+        for i in to_left:
+            answer(1, i)
+
+    for copy in (*mass_copies, *row_copies):
         copy.start()
 
     for a in (1, 2):
         weigh(a)
-    ends_out[0:8, :] = corners + (picked(1) + picked(2))
+    ends = corners + (picked(1) + picked(2))
+    for side in range(2):
+        sides_out[side, 0:4, :] = ends[4 * side : 4 * side + 4, :]
 
     @pl.when(jnp.logical_not(is_first))
     def _():
@@ -225,6 +236,7 @@
 
     load_win = load(win_hbm, win_ref, 11)
     load_wout = load(wout_hbm, wout_ref, 12)
+    load_cost = load(cost_hbm, cost_ref, 13)
 
     lane = lax.broadcasted_iota(jnp.int32, (1, across), 1)
     takes_before = (lane % 4 == 0) & (lane > 0)
@@ -254,12 +266,14 @@
     win_t_ref[...] = win_ref[...].T
     load_wout.wait()
     wout_t_ref[...] = wout_ref[...].T
+    load_cost.wait()
+    cost_out_ref[...] = jnp.concatenate([cost_ref[0:1, :], cost_ref[1:2, :]], axis=1)
 
     for copy in mass_copies:
         copy.wait_recv()
-    own = [mass_ref[a : a + 1, :] for a in range(4)]
-    own[0] = own[0] + mass_in[FROM_UP, 3:4, :]
-    own[3] = own[3] + mass_in[FROM_DOWN, 0:1, :]
+    own[0] = own[0] + mass_in[FROM_UP]
+    own[3] = own[3] + mass_in[FROM_DOWN]
+    mass_ends = jnp.concatenate(outermost(own), axis=0)
 
     def joined(value):
         earlier = pltpu.roll(value, 1, 1)
@@ -291,31 +305,25 @@
             if remap_ints[p][a]:
                 term = remap_ints[p][a] * updated
                 mixed[p] = term if mixed[p] is None else mixed[p] + term
+    ends = ends + (picks(0, rows_in[FROM_UP]) + picks(3, rows_in[FROM_DOWN]))
     for p in range(2):
         cells_ref[:, p * half : (p + 1) * half] = cells(mixed[p])
 
-    for copy in end_copies:
+    for copy in end_copies.values():
         copy.wait_recv()
 
-    def assembled(mine, first):
-        def row(i, r):
-            return ends_in[i, first + r : first + r + 1, :]
-
-        lines = []
-        for side, lateral, upper, lower in (
-            (0, FROM_LEFT, FROM_UL, FROM_DL), (1, FROM_RIGHT, FROM_UR, FROM_DR)
-        ):
-            near, far = 4 * side, 4 - 4 * side
-            for a in range(4):
-                line = mine[near + a : near + a + 1, :] + row(lateral, far + a)
-                if a == 0:
-                    line = line + (row(FROM_UP, near + 3) + row(upper, far + 3))
-                if a == 3:
-                    line = line + (row(FROM_DOWN, near) + row(lower, far))
-                lines.append(line)
-        return jnp.concatenate(lines, axis=0)
-
-    change = assembled(ends_out[0:8, :], 0) * (time_step / assembled(ends_out[8:16, :], 8))
+    def assembled(mine, first, line):
+        none = jnp.zeros((2, 2 * levels), jnp.float32)
+        upper_left, upper_right, lower_left, lower_right = (
+            corners_in[i - 4, line : line + 1, :] for i in (FROM_UL, FROM_UR, FROM_DL, FROM_DR)
+        )
+        sides = jnp.concatenate([sides_in[side, first : first + 4, :] for side in range(2)], axis=0)
+        diagonal = jnp.concatenate(
+            [upper_left, none, lower_left, upper_right, none, lower_right], axis=0
+        )
+        return mine + (sides + diagonal)
+
+    change = assembled(ends, 0, 0) * (time_step / assembled(mass_ends, 4, 1))
     high = change.astype(jnp.bfloat16).astype(jnp.float32)
     parts = jnp.concatenate([high, change - high], axis=0).T.astype(jnp.bfloat16)
     final = cells_ref[...] + dot(parts, place_ref[:, 4 * across :])
@@ -323,7 +331,7 @@
     for a in range(4):
         next_ref[a] = next_ref[a] + dot(parts, place_ref[:, a * across : (a + 1) * across])
 
-    for copy in (*mass_copies, *row_copies, *end_copies):
+    for copy in (*mass_copies, *row_copies, *end_copies.values()):
         copy.wait_send()
 
 
@@ -333,10 +341,8 @@
 
 
 def columns_kernel(
-    rows_ref, start_ref, cost_hbm, win_ref, wout_ref, next_hbm, cols_ref, cost_ref, load_sem, store_sem
+    rows_ref, start_ref, win_ref, wout_ref, cost_ref, next_hbm, cols_ref, state_ref, paired_ref, store_sem
 ):
-    load_cost = pltpu.make_async_copy(cost_hbm, cost_ref, load_sem)
-    load_cost.start()
     levels = next_hbm.shape[1]
     stores = [
         pltpu.make_async_copy(
@@ -347,22 +353,26 @@
     for copy in stores:
         copy.start()
     hidden_size, features = win_ref.shape
-    half = cost_ref.shape[1]
+    half = cols_ref.shape[1]
     chunk = hidden_size // 4
-    current = start_ref[...].astype(jnp.float32)
-    for step in range(3):
-        inputs = current.astype(jnp.bfloat16)
+    state_ref[...] = start_ref[...].astype(jnp.float32)
+
+    def substep(step, carry):
+        inputs = state_ref[...].astype(jnp.bfloat16)
         change = None
         for c in range(4):
             part = slice(c * chunk, (c + 1) * chunk)
             hidden = doubled_gelu(dot(win_ref[part, :], inputs)).astype(jnp.bfloat16)
             term = dot(wout_ref[:, part], hidden)
             change = term if change is None else change + term
-        if step == 0:
-            load_cost.wait()
-            cost = jnp.concatenate([cost_ref[0:1, :], cost_ref[1:2, :]], axis=1)
-        current = current + jnp.where(cost > step, 0.5, 0.0) * change
-    cols_ref[...] = jnp.stack([current[:, :half], current[:, half:]], axis=1).astype(jnp.bfloat16)
+        state_ref[...] += jnp.where(cost_ref[...] > step, 0.5, 0.0) * change
+        return carry
+
+    lax.fori_loop(0, 3, substep, 0)
+    current = state_ref[...]
+    paired_ref[0::2, :] = current[:, :half]
+    paired_ref[1::2, :] = current[:, half:]
+    cols_ref[...] = paired_ref[...].astype(jnp.bfloat16)
     for copy in stores:
         copy.wait()
 
@@ -377,17 +387,18 @@
     rows = (extent, channels, across)
     tables = constants(across)
     columns = column_cost.size
-    operands = (tracers, winds, node_mass, *map(jnp.asarray, tables), weight_in, weight_out)
-    next_rows, start, win_t, wout_t = pl.pallas_call(
+    operands = (tracers, winds, node_mass, *map(jnp.asarray, tables), weight_in, weight_out, column_cost)
+    next_rows, start, win_t, wout_t, cost = pl.pallas_call(
         functools.partial(kernel, sizes),
         out_shape=(
             jax.ShapeDtypeStruct(rows, f32),
             jax.ShapeDtypeStruct((features, columns), bf16),
             jax.ShapeDtypeStruct((hidden, features), bf16),
             jax.ShapeDtypeStruct((features, hidden), bf16),
+            jax.ShapeDtypeStruct((1, columns), column_cost.dtype),
         ),
-        in_specs=[hbm] * 10,
-        out_specs=(vmem,) * 4,
+        in_specs=[hbm] * 11,
+        out_specs=(vmem,) * 5,
         scratch_shapes=[
             pltpu.VMEM((extent, 2, levels, across), f32),
             pltpu.VMEM(winds.shape, bf16),
@@ -395,17 +406,20 @@
             *[pltpu.VMEM(table.shape, bf16) for table in tables],
             pltpu.VMEM(weight_in.shape, bf16),
             pltpu.VMEM(weight_out.shape, bf16),
+            pltpu.VMEM(column_cost.shape, column_cost.dtype),
             pltpu.VMEM(rows, f32),
             pltpu.VMEM((channels, across), f32),
             pltpu.VMEM((2, channels, across), bf16),
             pltpu.VMEM((2, channels, across), bf16),
-            pltpu.VMEM((16, channels), f32),
-            pltpu.VMEM((16, channels), f32),
-            pltpu.VMEM((8, 16, channels), f32),
-            pltpu.VMEM((2, extent, across), f32),
-            pltpu.SemaphoreType.DMA((13,)),
-            pltpu.SemaphoreType.DMA((12,)),
-            pltpu.SemaphoreType.DMA((12,)),
+            pltpu.VMEM((4, 2, channels), f32),
+            pltpu.VMEM((4, 2, channels), f32),
+            pltpu.VMEM((2, 8, channels), f32),
+            pltpu.VMEM((2, 8, channels), f32),
+            pltpu.VMEM((2, 1, across), f32),
+            pltpu.VMEM((2, 1, across), f32),
+            pltpu.SemaphoreType.DMA((14,)),
+            pltpu.SemaphoreType.DMA((10,)),
+            pltpu.SemaphoreType.DMA((10,)),
             pltpu.SemaphoreType.REGULAR((2,)),
         ],
         compiler_params=pltpu.CompilerParams(
@@ -419,17 +433,17 @@
         columns_kernel,
         out_shape=(
             jax.ShapeDtypeStruct(tracers.shape, f32),
-            jax.ShapeDtypeStruct((features, 2, across // 2), bf16),
+            jax.ShapeDtypeStruct((2 * features, across // 2), bf16),
         ),
-        in_specs=[vmem, vmem, hbm, vmem, vmem],
+        in_specs=[vmem] * 5,
         out_specs=(hbm, vmem),
         scratch_shapes=[
-            pltpu.VMEM(column_cost.shape, column_cost.dtype),
-            pltpu.SemaphoreType.DMA,
+            pltpu.VMEM((features, columns), f32),
+            pltpu.VMEM((2 * features, across // 2), f32),
             pltpu.SemaphoreType.DMA((4, 2)),
         ],
         compiler_params=pltpu.CompilerParams(vmem_limit_bytes=24 * 2**20),
-    )(next_rows, start, pltpu.with_memory_space_constraint(column_cost, pltpu.HBM), win_t, wout_t)
+    )(next_rows, start, win_t, wout_t, cost)
     return tracers_next, cols.reshape(4, levels, 2, across // 2)
 
 

time: 14.9 us -> 13.9 us (0.933)
  Pallas kernels: 14.1 us -> 13.1 us
    pallas_call x1, Pallas kernels: 11.1 us -> 10.2 us  [shards(): pl.pallas_call(functools.partial(kernel, sizes), out_shape=(jax.ShapeDtyp...]
where the time goes in v2:
time: 13.9 us; the launch traced here: 13.8 us
  Pallas kernels  13.1 us (94%)
  between operations  0.64 us (5%)
    pallas_call x1, Pallas kernels, shards(): pl.pallas_call(functools.partial(kernel, sizes), out_shape=(jax.ShapeDtyp...  10.2 us
    pallas_call x1, Pallas kernels, shards(): pl.pallas_call(columns_kernel, out_shape=(jax.ShapeDtypeStruct(tracers.sh...  2.89 us

profile of v2, /device:TPU:0, one launch (start us, length us, event | category | flops | bytes accessed | tf_op | source)
XLA Modules:
  0.0 13.8 jit_solution(1691978205472045060)
XLA Ops:
  0.6 10.2 %shard_map.122 = (f32[4,128,256]{2,1,0:T(8,128)S(1)}, bf16[256,256]{1,0:T(8,128)(2,1)S(1)}, bf16[1024,256]{1,0:T(8,128)(2,1)S(1)}, bf16[256,1024]{1,0:T(8,128)(2,1)S(1)}, s32[1,256]{1,0:T(1,128)S(1)}) custom-call(f32[2,64,4,256]{3,2,1,0:T(4,128)} %tracers_hbm.1, bf16[2,64,4,256]{3,2,1,0:T(4,128)(2,1)} %winds_hbm.1, f32[4,256]{1,0:T(4,128)} %mass_hbm.1, ...), custom_call_target="tpu_custom_call" | custom-call | flops 1000000000 | bytes 4194304 | tf_op jit(solution)/shard_map/pallas_call | solution.py:391
  10.9 2.9 %shard_map.123 = (f32[2,64,4,256]{3,2,1,0:T(4,128)}, bf16[512,128]{1,0:T(8,128)(2,1)}) custom-call(f32[4,128,256]{2,1,0:T(8,128)S(1)} %get-tuple-element.9.rows_ref, bf16[256,256]{1,0:T(8,128)(2,1)S(1)} %get-tuple-element.10.start_ref, bf16[1024,256]{1,0:T(8,128)(2,1)S(1)} %get-tuple-element.11.win_ref, bf16[256,1024]{1,0:T(8,128)(2,1)S(1)} %get-tuple-element.12.wout_ref, ...), custom_call_target="tpu_custom_call" | custom-call | tf_op jit(solution)/shard_map/pallas_call | solution.py:432

commit v3 on v2

--- a/solution.py
+++ b/solution.py
@@ -350,25 +350,21 @@
         )
         for a in range(4) for k in range(2)
     ]
-    for copy in stores:
-        copy.start()
-    hidden_size, features = win_ref.shape
+    features = win_ref.shape[1]
     half = cols_ref.shape[1]
-    chunk = hidden_size // 4
     state_ref[...] = start_ref[...].astype(jnp.float32)
 
-    def substep(step, carry):
+    def substep(step):
         inputs = state_ref[...].astype(jnp.bfloat16)
-        change = None
-        for c in range(4):
-            part = slice(c * chunk, (c + 1) * chunk)
-            hidden = doubled_gelu(dot(win_ref[part, :], inputs)).astype(jnp.bfloat16)
-            term = dot(wout_ref[:, part], hidden)
-            change = term if change is None else change + term
+        hidden = doubled_gelu(dot(win_ref[...], inputs)).astype(jnp.bfloat16)
+        change = dot(wout_ref[...], hidden)
         state_ref[...] += jnp.where(cost_ref[...] > step, 0.5, 0.0) * change
-        return carry
-
-    lax.fori_loop(0, 3, substep, 0)
+
+    for step in range(3):
+        substep(step)
+        if step == 0:
+            for copy in stores:
+                copy.start()
     current = state_ref[...]
     paired_ref[0::2, :] = current[:, :half]
     paired_ref[1::2, :] = current[:, half:]

time: 13.9 us -> 13.6 us (0.978)
  Pallas kernels: 13.1 us -> 12.8 us
    pallas_call x1, Pallas kernels: 2.89 us -> 2.57 us  [shards(): pl.pallas_call(columns_kernel, out_shape=(jax.ShapeDtypeStruct(tracers.sh...]
where the time goes in v3:
time: 13.6 us; the launch traced here: 13.4 us
  Pallas kernels  12.8 us (94%)
  between operations  0.64 us (5%)
    pallas_call x1, Pallas kernels, shards(): pl.pallas_call(functools.partial(kernel, sizes), out_shape=(jax.ShapeDtyp...  10.2 us
    pallas_call x1, Pallas kernels, shards(): pl.pallas_call(columns_kernel, out_shape=(jax.ShapeDtypeStruct(tracers.sh...  2.57 us

profile of v3, /device:TPU:0, one launch (start us, length us, event | category | flops | bytes accessed | tf_op | source)
XLA Modules:
  0.0 13.4 jit_solution(13294652930483951998)
XLA Ops:
  0.6 10.2 %shard_map.122 = (f32[4,128,256]{2,1,0:T(8,128)S(1)}, bf16[256,256]{1,0:T(8,128)(2,1)S(1)}, bf16[1024,256]{1,0:T(8,128)(2,1)S(1)}, bf16[256,1024]{1,0:T(8,128)(2,1)S(1)}, s32[1,256]{1,0:T(1,128)S(1)}) custom-call(f32[2,64,4,256]{3,2,1,0:T(4,128)} %tracers_hbm.1, bf16[2,64,4,256]{3,2,1,0:T(4,128)(2,1)} %winds_hbm.1, f32[4,256]{1,0:T(4,128)} %mass_hbm.1, ...), custom_call_target="tpu_custom_call" | custom-call | flops 1000000000 | bytes 4194304 | tf_op jit(solution)/shard_map/pallas_call | solution.py:387
  10.9 2.6 %shard_map.123 = (f32[2,64,4,256]{3,2,1,0:T(4,128)}, bf16[512,128]{1,0:T(8,128)(2,1)}) custom-call(f32[4,128,256]{2,1,0:T(8,128)S(1)} %get-tuple-element.9.rows_ref, bf16[256,256]{1,0:T(8,128)(2,1)S(1)} %get-tuple-element.10.start_ref, bf16[1024,256]{1,0:T(8,128)(2,1)S(1)} %get-tuple-element.11.win_ref, bf16[256,1024]{1,0:T(8,128)(2,1)S(1)} %get-tuple-element.12.wout_ref, ...), custom_call_target="tpu_custom_call" | custom-call | tf_op jit(solution)/shard_map/pallas_call | solution.py:428

commit v4 on v3

--- a/solution.py
+++ b/solution.py
@@ -82,7 +82,8 @@
     n_grp, n_bal = sizes
     levels, across = winds_ref.shape[1], winds_ref.shape[3]
     grp, bal = lax.axis_index("grp"), lax.axis_index("bal")
-    is_first, is_last = bal == 0, bal == n_bal - 1
+    is_end = jnp.logical_or(bal == 0, bal == n_bal - 1)
+    is_late = bal >= n_bal - 2
 
     def peer(i):
         dg, db = DIRS[i]
@@ -113,15 +114,23 @@
     for i in range(2):
         greet(i)
 
-    @pl.when(is_first)
+    @pl.when(is_end)
     def _():
         for i in to_left:
             greet(i)
 
-    @pl.when(jnp.logical_not(is_last))
+    @pl.when(jnp.logical_not(is_late))
     def _():
         for i in to_right:
             greet(i)
+
+    node = lax.broadcasted_iota(jnp.int32, (levels, 4 * levels), 1)
+    level = lax.broadcasted_iota(jnp.int32, (levels, 4 * levels), 0)
+
+    def selection(first, second):
+        return jnp.concatenate(
+            [jnp.where(node == 4 * level + a, 1.0, 0.0) for a in (first, second)], axis=0
+        ).astype(jnp.bfloat16)
 
     load_mass.wait()
 
@@ -145,18 +154,20 @@
 
     derivative = gll_matrix()
 
-    def weigh(a):
+    def blown(first, second):
+        rows = selection(first, second)
+        return [dot(rows, winds_ref[k].reshape(4 * levels, across)) for k in range(2)]
+
+    def weigh(a, winds):
         here = tracer_row(a)
         high, low = split(here)
         along_y = dot(high, dhigh_ref[...]) + dot(low, dhigh_ref[...]) + dot(high, dlow_ref[...])
         along_x = sum(float(derivative[a, c]) * tracer_row(c) for c in range(4))
-        first = winds_ref[0, :, a, :].astype(jnp.float32)
-        second = winds_ref[1, :, a, :].astype(jnp.float32)
-        mass = mass_ref[a : a + 1, :]
-        first, second = first * mass, second * mass
+        mass = -mass_ref[a : a + 1, :]
+        first, second = winds[0] * mass, winds[1] * mass
         for k in range(2):
             part = slice(k * levels, (k + 1) * levels)
-            weighted[a, part, :] = -(first * along_x[part] + second * along_y[part])
+            weighted[a, part, :] = first * along_x[part] + second * along_y[part]
 
     def picks(a, value):
         return lax.dot_general(
@@ -166,8 +177,12 @@
     def picked(a):
         return picks(a, weighted[a].astype(jnp.bfloat16))
 
-    for a in (0, 3):
-        weigh(a)
+    def weigh_pair(first, second):
+        winds = blown(first, second)
+        weigh(first, [wind[:levels] for wind in winds])
+        weigh(second, [wind[levels:] for wind in winds])
+
+    weigh_pair(0, 3)
     rows_out[0] = weighted[3].astype(jnp.bfloat16)
     rows_out[1] = weighted[0].astype(jnp.bfloat16)
     load_pick.wait()
@@ -189,13 +204,13 @@
         **{4 + c: remote(corners_out.at[c], corners_in.at[c], 6 + c, 4 + c) for c in range(4)},
     }
 
-    before = jnp.where(bal > 0, 3, 0) + jnp.where(is_last, 3, 0)
+    before = jnp.where(bal > 0, 3, 0) + jnp.where(bal == n_bal - 2, 3, 0)
     pl.semaphore_wait(barrier, 2 + before)
 
     def answer(slot, i):
         pl.semaphore_signal(ack_sem.at[slot], inc=1, device_id=peer(i), device_id_type=MESH)
 
-    @pl.when(is_last)
+    @pl.when(is_late)
     def _():
         for i in to_right:
             if i > 3:
@@ -203,7 +218,7 @@
         for i in to_right:
             answer(0, i)
 
-    @pl.when(jnp.logical_not(is_first))
+    @pl.when(jnp.logical_not(is_end))
     def _():
         for i in to_left:
             if i > 3:
@@ -214,21 +229,20 @@
     for copy in (*mass_copies, *row_copies):
         copy.start()
 
-    for a in (1, 2):
-        weigh(a)
+    weigh_pair(1, 2)
     ends = corners + (picked(1) + picked(2))
     for side in range(2):
         sides_out[side, 0:4, :] = ends[4 * side : 4 * side + 4, :]
 
-    @pl.when(jnp.logical_not(is_first))
+    @pl.when(jnp.logical_not(is_end))
     def _():
         end_copies[3].start()
 
-    @pl.when(is_last)
+    @pl.when(is_late)
     def _():
         end_copies[2].start()
 
-    @pl.when(jnp.logical_not(is_last))
+    @pl.when(jnp.logical_not(is_late))
     def _():
         pl.semaphore_wait(ack_sem.at[1], 3)
         for i in to_right:
@@ -284,7 +298,7 @@
 
     load_place.wait()
 
-    @pl.when(is_first)
+    @pl.when(is_end)
     def _():
         pl.semaphore_wait(ack_sem.at[0], 3)
         for i in to_left:
@@ -300,7 +314,7 @@
         if a == 3:
             value = value + rows_in[FROM_DOWN].astype(jnp.float32)
         updated = tracer_row(a) + scales[a] * joined(value)
-        next_ref[a] = updated
+        next_ref[a] = updated.reshape(2, levels, across)
         for p in range(2):
             if remap_ints[p][a]:
                 term = remap_ints[p][a] * updated
@@ -329,7 +343,8 @@
     final = cells_ref[...] + dot(parts, place_ref[:, 4 * across :])
     start_ref[0 : 2 * levels, :] = (final * (1.0 / 400.0)).astype(jnp.bfloat16)
     for a in range(4):
-        next_ref[a] = next_ref[a] + dot(parts, place_ref[:, a * across : (a + 1) * across])
+        late = dot(parts, place_ref[:, a * across : (a + 1) * across])
+        next_ref[a] = next_ref[a] + late.reshape(2, levels, across)
 
     for copy in (*mass_copies, *row_copies, *end_copies.values()):
         copy.wait_send()
@@ -343,12 +358,9 @@
 def columns_kernel(
     rows_ref, start_ref, win_ref, wout_ref, cost_ref, next_hbm, cols_ref, state_ref, paired_ref, store_sem
 ):
-    levels = next_hbm.shape[1]
     stores = [
-        pltpu.make_async_copy(
-            rows_ref.at[a, pl.ds(k * levels, levels), :], next_hbm.at[k, :, a, :], store_sem.at[a, k]
-        )
-        for a in range(4) for k in range(2)
+        pltpu.make_async_copy(rows_ref.at[a], next_hbm.at[:, :, a, :], store_sem.at[a])
+        for a in range(4)
     ]
     features = win_ref.shape[1]
     half = cols_ref.shape[1]
@@ -387,7 +399,7 @@
     next_rows, start, win_t, wout_t, cost = pl.pallas_call(
         functools.partial(kernel, sizes),
         out_shape=(
-            jax.ShapeDtypeStruct(rows, f32),
+            jax.ShapeDtypeStruct((extent, 2, levels, across), f32),
             jax.ShapeDtypeStruct((features, columns), bf16),
             jax.ShapeDtypeStruct((hidden, features), bf16),
             jax.ShapeDtypeStruct((features, hidden), bf16),
@@ -436,7 +448,7 @@
         scratch_shapes=[
             pltpu.VMEM((features, columns), f32),
             pltpu.VMEM((2 * features, across // 2), f32),
-            pltpu.SemaphoreType.DMA((4, 2)),
+            pltpu.SemaphoreType.DMA((4,)),
         ],
         compiler_params=pltpu.CompilerParams(vmem_limit_bytes=24 * 2**20),
     )(next_rows, start, win_t, wout_t, cost)

time: 13.6 us -> 13.5 us (level)
  no operation moved by 1% of the time
where the time goes in v4:
time: 13.5 us; the launch traced here: 13.3 us
  Pallas kernels  12.7 us (94%)
  between operations  0.64 us (5%)
    pallas_call x1, Pallas kernels, shards(): pl.pallas_call(functools.partial(kernel, sizes), out_shape=(jax.ShapeDtyp...  10.2 us
    pallas_call x1, Pallas kernels, shards(): pl.pallas_call(columns_kernel, out_shape=(jax.ShapeDtypeStruct(tracers.sh...  2.53 us

profile of v4, /device:TPU:0, one launch (start us, length us, event | category | flops | bytes accessed | tf_op | source)
XLA Modules:
  0.0 13.3 jit_solution(8475185380084724990)
XLA Ops:
  0.6 10.2 %shard_map.122 = (f32[4,2,64,256]{3,2,1,0:T(8,128)S(1)}, bf16[256,256]{1,0:T(8,128)(2,1)S(1)}, bf16[1024,256]{1,0:T(8,128)(2,1)S(1)}, bf16[256,1024]{1,0:T(8,128)(2,1)S(1)}, s32[1,256]{1,0:T(1,128)S(1)}) custom-call(f32[2,64,4,256]{3,2,1,0:T(4,128)} %tracers_hbm.1, bf16[2,64,4,256]{3,2,1,0:T(4,128)(2,1)} %winds_hbm.1, f32[4,256]{1,0:T(4,128)} %mass_hbm.1, ...), custom_call_target="tpu_custom_call" | custom-call | flops 1000000000 | bytes 4194304 | tf_op jit(solution)/shard_map/pallas_call | solution.py:399
  10.8 2.5 %shard_map.123 = (f32[2,64,4,256]{3,2,1,0:T(4,128)}, bf16[512,128]{1,0:T(8,128)(2,1)}) custom-call(f32[4,2,64,256]{3,2,1,0:T(8,128)S(1)} %get-tuple-element.9.rows_ref, bf16[256,256]{1,0:T(8,128)(2,1)S(1)} %get-tuple-element.10.start_ref, bf16[1024,256]{1,0:T(8,128)(2,1)S(1)} %get-tuple-element.11.win_ref, bf16[256,1024]{1,0:T(8,128)(2,1)S(1)} %get-tuple-element.12.wout_ref, ...), custom_call_target="tpu_custom_call" | custom-call | tf_op jit(solution)/shard_map/pallas_call | solution.py:440

commit v5 on v4

--- a/solution.py
+++ b/solution.py
@@ -226,7 +226,7 @@
         for i in to_left:
             answer(1, i)
 
-    for copy in (*mass_copies, *row_copies):
+    for copy in (*row_copies, *mass_copies):
         copy.start()
 
     weigh_pair(1, 2)

time: 13.5 us -> 14.8 us (1.096)
  the two profiles are of different devices: /device:TPU:0 before, /device:TPU:25 now
where the time goes in v5:
time: 14.8 us; the launch traced here: 14.6 us
  Pallas kernels  13.9 us (94%)
  between operations  0.64 us (4%)
    pallas_call x1, Pallas kernels, shards(): pl.pallas_call(functools.partial(kernel, sizes), out_shape=(jax.ShapeDtyp...  11.4 us
    pallas_call x1, Pallas kernels, shards(): pl.pallas_call(columns_kernel, out_shape=(jax.ShapeDtypeStruct(tracers.sh...  2.53 us

profile of v5, /device:TPU:25, one launch (start us, length us, event | category | flops | bytes accessed | tf_op | source)
XLA Modules:
  0.0 14.6 jit_solution(6161311869264116219)
XLA Ops:
  0.6 11.4 %shard_map.122 = (f32[4,2,64,256]{3,2,1,0:T(8,128)S(1)}, bf16[256,256]{1,0:T(8,128)(2,1)S(1)}, bf16[1024,256]{1,0:T(8,128)(2,1)S(1)}, bf16[256,1024]{1,0:T(8,128)(2,1)S(1)}, s32[1,256]{1,0:T(1,128)S(1)}) custom-call(f32[2,64,4,256]{3,2,1,0:T(4,128)} %tracers_hbm.1, bf16[2,64,4,256]{3,2,1,0:T(4,128)(2,1)} %winds_hbm.1, f32[4,256]{1,0:T(4,128)} %mass_hbm.1, ...), custom_call_target="tpu_custom_call" | custom-call | flops 1000000000 | bytes 4194304 | tf_op jit(solution)/shard_map/pallas_call | solution.py:399
  12.0 2.5 %shard_map.123 = (f32[2,64,4,256]{3,2,1,0:T(4,128)}, bf16[512,128]{1,0:T(8,128)(2,1)}) custom-call(f32[4,2,64,256]{3,2,1,0:T(8,128)S(1)} %get-tuple-element.9.rows_ref, bf16[256,256]{1,0:T(8,128)(2,1)S(1)} %get-tuple-element.10.start_ref, bf16[1024,256]{1,0:T(8,128)(2,1)S(1)} %get-tuple-element.11.win_ref, bf16[256,1024]{1,0:T(8,128)(2,1)S(1)} %get-tuple-element.12.wout_ref, ...), custom_call_target="tpu_custom_call" | custom-call | tf_op jit(solution)/shard_map/pallas_call | solution.py:440
